TPU v7x, 32 devices: a whole 2x2x4 slice. The times are simulated.
32 devices in a mesh: groups: 2 (over y), rows: 4 (over z), cols: 2 (over x), sub: 2 (over core).
Axes of the slice: x: 2, y: 2, z: 4, core: 2. Of those that a mesh axis runs over, the one named last changes fastest.
Arguments:
- tile_index: int32 [64, 2], P(('groups', 'rows', 'cols', 'sub')), parts along dimension 0, may hold values from 0 to 7, as said below
- tile_values: bfloat16 [64, 256, 256], P(('groups', 'rows', 'cols', 'sub')), parts along dimension 0, may hold values from -0.125 to 0.125
- onsite_energy: float32 [4096], P(('groups', 'rows', 'cols')), parts along dimension 0, may hold values from 0.5 to 4
- start_block: float32 [4096, 64], P(('groups', 'rows', 'cols')), parts along dimension 0, may hold values from -6 to 6
- previous_block: float32 [4096, 64], P(('groups', 'rows', 'cols')), parts along dimension 0, may hold values from -6 to 6
- previous_coupling: float32 [128, 64], P('groups'), parts along dimension 0, may hold values from -0.6 to 0.6
- stored_basis: float32 [8, 4096, 64], P('sub', ('groups', 'rows', 'cols')), parts along dimension 1, may hold values from -6 to 6
Outputs:
- new_blocks: float32 [1, 4096, 64], P(None, ('groups', 'rows', 'cols')), parts along dimension 1
- diagonal_blocks: float32 [1, 128, 64], P(None, 'groups'), parts along dimension 1
- coupling_blocks: float32 [1, 128, 64], P(None, 'groups'), parts along dimension 1
There are 2 independent parts, one for each index of `groups`. A program takes and returns all parts, laid end to end along the dimension named above; each array names one. Nothing has to cross between parts.
Inputs may be any that keep to these rules, and one draw needn't show every extreme that they name: `tile_index`: tile rows of a device's tiles lie in the rows of the operator that the device's index of rows and cols holds; tile columns lie in the rows held by some index of rows with the same index of cols. Tiles may repeat.
All inputs are finite; a program needn't handle non-finite values.
Results may differ from a plain program's by a relative error of at most 0.0019.
Values may be sent and summed in bfloat16 or wider, within the bound.
A program may use at most 64 MiB of HBM per device.

v0:
```python
import jax
import jax.numpy as jnp
from jax import lax
from jax.sharding import PartitionSpec as P

BLOCK = 64
TILE = 256


highest = lax.Precision.HIGHEST


def apply_operator(tile_index, tile_values, onsite_energy, current):
    local_rows = current.shape[0]
    tile_rows = local_rows // TILE
    band_count = lax.axis_size("rows")
    column_count = lax.axis_size("cols")
    narrow = current.astype(jnp.bfloat16)
    own_tiles = narrow.reshape(tile_rows, TILE, BLOCK)
    local_row = tile_index[:, 0] % tile_rows
    column = tile_index[:, 1]
    source = column // tile_rows // column_count * tile_rows + column % tile_rows
    gathered = lax.all_gather(own_tiles, "rows", axis=0, tiled=True)
    pulled = jnp.einsum(
        "kab,kbn->kan", tile_values, gathered[source], preferred_element_type=jnp.float32
    )
    pushed = jnp.einsum(
        "kab,kan->kbn", tile_values, own_tiles[local_row], preferred_element_type=jnp.float32
    )
    slot_count = band_count * tile_rows
    slot_range = jnp.arange(slot_count, dtype=jnp.int32)
    push_onehot = (source[None, :] == slot_range[:, None]).astype(jnp.float32)
    terms = jnp.einsum("sk,kbn->sbn", push_onehot, pushed, precision=highest)
    received = lax.psum_scatter(terms, "rows", scatter_dimension=0, tiled=True)
    row_onehot = (local_row[None, :] == jnp.arange(tile_rows, dtype=jnp.int32)[:, None]).astype(
        jnp.float32
    )
    partial_total = received + jnp.einsum("tk,kan->tan", row_onehot, pulled, precision=highest)
    total = lax.psum(partial_total, "sub")
    return total.reshape(local_rows, BLOCK) + onsite_energy[:, None] * current


def local(
    tile_index,
    tile_values,
    onsite_energy,
    start_block,
    previous_block,
    previous_coupling,
    stored_basis,
):
    local_rows = start_block.shape[0]
    total_rows = local_rows * lax.axis_size("rows") * lax.axis_size("cols")
    coupling = jnp.triu(previous_coupling)
    correlation_local = jnp.einsum("kib,ic->kbc", stored_basis, start_block, precision=highest)
    correlation = lax.psum(correlation_local, ("rows", "cols")) / total_rows
    images = apply_operator(tile_index, tile_values, onsite_energy, start_block)
    images = images - jnp.dot(previous_block, coupling.T, precision=highest)
    diagonal_local = jnp.dot(start_block.T, images, precision=highest)
    stored_local = jnp.einsum("kib,ic->kbc", stored_basis, images, precision=highest)
    raw_diagonal, raw_stored = lax.psum((diagonal_local, stored_local), ("rows", "cols"))
    diagonal = raw_diagonal / total_rows
    projection = raw_stored / total_rows - jnp.einsum(
        "kbc,cd->kbd", correlation, diagonal, precision=highest
    )
    images = images - jnp.dot(start_block, diagonal, precision=highest)
    removal_local = jnp.einsum("kib,kbc->ic", stored_basis, projection, precision=highest)
    removal = lax.psum(removal_local, "sub")
    images = images - removal
    gram_local = jnp.dot(images.T, images, precision=highest)
    gram = lax.psum(gram_local, ("rows", "cols")) / total_rows
    lower_factor = jnp.linalg.cholesky(gram)
    following = lax.linalg.triangular_solve(
        lower_factor, images, left_side=False, lower=True, transpose_a=True
    )
    new_list = [following]
    diagonal_list = [diagonal]
    coupling_list = [lower_factor.T]
    return (jnp.stack(new_list), jnp.stack(diagonal_list), jnp.stack(coupling_list))


def solution(mesh):
    return jax.shard_map(
        local,
        mesh=mesh,
        in_specs=(
            P(("groups", "rows", "cols", "sub"), None),
            P(("groups", "rows", "cols", "sub"), None, None),
            P(("groups", "rows", "cols")),
            P(("groups", "rows", "cols"), None),
            P(("groups", "rows", "cols"), None),
            P("groups", None),
            P("sub", ("groups", "rows", "cols"), None),
        ),
        out_specs=(
            P(None, ("groups", "rows", "cols"), None),
            P(None, "groups", None),
            P(None, "groups", None),
        ),
        check_vma=False,
    )
```

profile of v0, /device:TPU:0, one launch (start us, length us, event | category | flops | bytes accessed | tf_op | source)
XLA Modules:
  0.0 217.6 jit_solution(17785886655713540770)
XLA Ops:
  7.2 0.9 convert_element_type.2
  8.1 0.9 fusion.27
  9.0 0.2 fusion.15
  9.2 0.5 fusion.5
  9.7 0.8 copy.31
  10.6 15.6 %all-gather = bf16[1024,64]{0,1:T(8,128)(2,1)S(1)} all-gather(bf16[256,64]{0,1:T(8,128)(2,1)S(1)} %convert_element_type.2), channel_id=2, replica_groups=mesh['groups'=2,'rows'=4,'cols'=2,'sub'=2] {'rows'}, dimensions={0}, use_global_device_ids=true | all-gather | bytes 163840 | tf_op jit(solution)/shard_map/all_gather | solution.py:23
  26.2 0.6 gather_fusion
  26.8 0.2 convolution_bitcast_fusion.1
  27.0 9.0 %fusion.3 = f32[1,256,64]{0,1,2:T(8,128)} fusion(f32[2,256,64]{1,2,0:T(8,128)S(1)} %convolution_bitcast_fusion.1), kind=kOutput, calls=%fused_computation.13 | convolution fusion | flops 393216 | bytes 196608 | tf_op jit(solution)/shard_map/tk,kan->tan/dot_general | solution.py:38
  36.0 5.2 %copy.42 = f32[1,256,64]{1,2,0:T(8,128)S(1)} copy(f32[1,256,64]{0,1,2:T(8,128)} %fusion.3) | data formatting | bytes 131072 | tf_op jit(solution)/shard_map/tk,kan->tan/dot_general | solution.py:38
  41.2 1.2 fusion.8
  42.4 1.5 add_bitcast_fusion
  43.9 18.8 %all-reduce.5.cloned.1.call-done = f32[256,64]{0,1:T(8,128)} async-done(((f32[256,64]{0,1:T(8,128)}), f32[256,64]{0,1:T(8,128)}) %all-reduce.5.cloned.1.call-update) | async-done | bytes 65552 | tf_op jit(solution)/shard_map/psum | solution.py:39
  62.8 1.1 fusion.2
  63.9 1.2 convolution_bitcast_fusion
  65.1 0.2 convolution_bitcast_fusion.6
  65.3 37.4 %psum.43 = f32[64,64]{0,1:T(8,128)S(1)} all-reduce(f32[64,64]{0,1:T(8,128)S(1)} %convolution_bitcast_fusion.6), channel_id=1, replica_groups=mesh['groups'=2,'rows'=4,'cols'=2,'sub'=2] {'rows','cols'}, use_global_device_ids=true, to_apply=%region_2.3 | all-reduce | flops 4096 | bytes 32768 | tf_op jit(solution)/shard_map/psum | solution.py:61
  102.7 36.2 %all-reduce.9.cloned.1.call-done = (f32[4,64,64]{1,2,0:T(8,128)}, f32[4,64,64]{1,2,0:T(8,128)}) async-done(((f32[4,64,64]{1,2,0:T(8,128)}, f32[4,64,64]{1,2,0:T(8,128)}), (f32[4,64,64]{1,2,0:T(8,128)}, f32[4,64,64]{1,2,0:T(8,128)})) %all-reduce.9.cloned.1.call-update) | async-done | bytes 131088 | tf_op jit(solution)/shard_map/psum | solution.py:56
  138.9 1.2 convolution_subtract_fusion
  140.1 0.9 convolution_bitcast_fusion.5
  141.1 0.7 copy.39
  141.8 16.8 %all-reduce.7.cloned.1.call-done = f32[256,64]{0,1:T(8,128)} async-done(((f32[256,64]{0,1:T(8,128)}), f32[256,64]{0,1:T(8,128)}) %all-reduce.7.cloned.1.call-update) | async-done | bytes 65552 | tf_op jit(solution)/shard_map/psum | solution.py:68
  158.6 1.0 fusion.1
  159.7 0.2 fusion.35
  159.9 37.4 %psum.47 = f32[64,64]{0,1:T(8,128)S(1)} all-reduce(f32[64,64]{0,1:T(8,128)S(1)} %fusion.35), channel_id=1, replica_groups=mesh['groups'=2,'rows'=4,'cols'=2,'sub'=2] {'rows','cols'}, use_global_device_ids=true, to_apply=%region_6.7 | all-reduce | flops 4096 | bytes 32768 | tf_op jit(solution)/shard_map/psum | solution.py:71
  197.3 0.1 copy.38
  197.4 5.8 %cholesky.15 = f32[64,64]{1,0:T(8,128)S(1)} custom-call(f32[64,64]{1,0:T(8,128)S(1)} %fusion.13), custom_call_target="Cholesky" | custom-call | tf_op jit(solution)/shard_map/jit(cholesky)/cholesky | solution.py:72
  203.3 0.6 compare_reduce_fusion
  203.9 0.7 fusion.20
  204.6 4.9 %custom-call.6 = f32[1,64,64]{1,2,0:T(8,128)S(1)} custom-call(f32[1,64,64]{2,1,0:T(8,128)S(1)} %get-tuple-element.20), custom_call_target="InvertDiagBlocksLowerTriangular" | custom-call | tf_op jit(solution)/shard_map/triangular_solve | solution.py:73
  209.5 0.9 convolution_bitcast_fusion.2
  210.4 0.7 copy.40
  (29 shorter events, 0.4 us)
Async XLA Ops:
  7.2 1.9 copy-start
  7.2 35.2 %reduce-scatter.2.cloned.1.call-start = ((), (), s32[]{:S(2)}) async-start(), calls=%async_computation.1 | async-start | bytes 327680 | tf_op jit(solution)/shard_map/reduce_scatter | solution.py:34
  10.5 52.2 %all-reduce.5.cloned.1.call-start = ((), (), s32[]{:S(2)}) async-start(), calls=%async_computation.2 | async-start | bytes 131072 | tf_op jit(solution)/shard_map/psum | solution.py:39
  27.0 14.2 %copy-start.1 = (f32[4,256,64]{1,2,0:T(8,128)S(1)}, f32[4,256,64]{1,2,0:T(8,128)}, u32[]{:S(2)}) copy-start(f32[4,256,64]{1,2,0:T(8,128)} %param.13) | copy-start | bytes 786436
  27.0 14.2 %copy-start.2 = (f32[256,64]{0,1:T(8,128)S(1)}, f32[256,64]{0,1:T(8,128)}, u32[]{:S(2)}) copy-start(f32[256,64]{0,1:T(8,128)} %param.10) | copy-start | bytes 196612
  27.0 35.8 %copy-start.3 = (f32[256,64]{0,1:T(8,128)S(1)}, f32[256,64]{0,1:T(8,128)}, u32[]{:S(2)}) copy-start(f32[256,64]{0,1:T(8,128)} %param.11) | copy-start | bytes 196612
  27.0 35.7 %copy-start.4 = (f32[64,64]{1,0:T(8,128)S(1)}, f32[64,64]{1,0:T(8,128)}, u32[]{:S(2)}) copy-start(f32[64,64]{1,0:T(8,128)} %param.12) | copy-start | bytes 49156
  27.0 35.7 %copy-start.5 = (f32[256]{0:T(256)S(1)}, f32[256]{0:T(256)}, u32[]{:S(2)}) copy-start(f32[256]{0:T(256)} %param.9) | copy-start | bytes 3076
  43.9 95.0 %all-reduce.9.cloned.1.call-start = ((), (), s32[]{:S(2)}) async-start(), calls=%async_computation.4 | async-start | bytes 524288 | tf_op jit(solution)/shard_map/psum | solution.py:56
  65.0 93.6 %all-reduce.7.cloned.1.call-start = ((), (), s32[]{:S(2)}) async-start(), calls=%async_computation.3 | async-start | bytes 131072 | tf_op jit(solution)/shard_map/psum | solution.py:68
Sparse Core Ops, SparseCore 0:
  10.6 22.8 reduce-scatter.1
  44.0 18.7 all-reduce.4
  66.2 72.6 all-reduce.8
  141.6 16.9 all-reduce.6
where the time goes:
time: 218 us
  blocking collectives  90.4 us (41%)
  waiting for transfers between devices  71.9 us (33%)
  matrix products  17.8 us (8%)
  other arithmetic  15.4 us (7%)
  between operations  13.9 us (6%)
  local copies, waits for them, and re-layouts  8.02 us (4%)
    psum x1, blocking collectives, local(): gram = lax.psum(gram_local, ('rows', 'cols')) / total_rows  37.4 us
    psum x1, blocking collectives, local(): lax.psum((diagonal_local, stored_local), ('rows', 'cols'))  37.4 us
    psum x1, waiting for transfers between devices, local(): correlation = lax.psum(correlation_local, ('rows', 'cols')) / total_rows  36.2 us
    psum x1, waiting for transfers between devices, apply_operator(): total = lax.psum(partial_total, 'sub')  18.8 us
    psum x1, waiting for transfers between devices, local(): removal = lax.psum(removal_local, 'sub')  16.8 us
    all_gather x1, blocking collectives, apply_operator(): gathered = lax.all_gather(own_tiles, 'rows', axis=0, tiled=True)  15.6 us
    dot_general x1, matrix products, apply_operator(): jnp.einsum('tk,kan->tan', row_onehot, pulled, precision=highest)  8.95 us
    another operation x3, other arithmetic, local(): lower_factor = jnp.linalg.cholesky(gram)  6.52 us
  transfers between devices with their start and end apart: 4, of which 3 were waited for; matrix products, arithmetic and copies ran while one was open for 8% of the time, Pallas kernels for 0%

commit v1 on v0

v1 whole, which is shorter than its diff:
```python
import functools

import jax
import jax.numpy as jnp
from jax import lax
from jax.experimental import pallas as pl
from jax.experimental.pallas import tpu as pltpu
from jax.sharding import PartitionSpec as P

MESH = pl.DeviceIdType.MESH
NN = (((1,), (0,)), ((), ()))
NT = (((1,), (1,)), ((), ()))
CH = 16
LANES = 128


def split(x):
    high = x.astype(jnp.bfloat16)
    return high, (x - high.astype(jnp.float32)).astype(jnp.bfloat16)


def mm(a, b, dims):
    return lax.dot_general(a, b, dims, preferred_element_type=jnp.float32)


def dot3(a, b, dims):
    return mm(a[0], b[0], dims) + (mm(a[0], b[1], dims) + mm(a[1], b[0], dims))


def loop(lo, hi, body):
    if hi - lo <= 20:
        for i in range(lo, hi):
            body(i)
    else:
        lax.fori_loop(lo, hi, lambda i, c: (body(i), c)[1], 0)


def eliminate(full, block):
    count = block // 8
    parts = [full[8 * b:8 * b + 8] for b in range(count)]
    wide = (8, full.shape[1])
    sub_id = lax.broadcasted_iota(jnp.int32, wide, 0)
    done = []
    for b in range(count):
        rows = [jnp.broadcast_to(parts[b][p:p + 1], wide) for p in range(8)]
        cols = [
            [jnp.broadcast_to(parts[a][:, 8 * b + q:8 * b + q + 1], wide) for a in range(b, count)]
            for q in range(8)
        ]
        square = [[jnp.broadcast_to(cols[q][0][p:p + 1], wide) for q in range(8)] for p in range(8)]
        pivot = square[0][0]
        for p in range(8):
            inverse = 1.0 / square[p][p]
            for q in range(p + 1, 8):
                m = square[p][q] * inverse
                for t in range(q, 8):
                    square[q][t] = square[q][t] - m * square[p][t]
                rows[q] = rows[q] - m * rows[p]
            for i, a in enumerate(range(b, count)):
                factor = cols[p][i] * inverse
                if a == b:
                    factor = jnp.where(sub_id > p, factor, 0.0)
                for q in range(p + 1, 8):
                    cols[q][i] = cols[q][i] - factor * square[p][q]
                parts[a] = parts[a] - factor * rows[p]
            pivot = jnp.where(sub_id == p, square[p][p], pivot)
        done.append(parts[b] * lax.rsqrt(pivot))
    return jnp.concatenate(done, axis=0)


def kernel(
    dims, index_ref, tiles_in, onsite_ref, start_in, previous_in, coupling_ref, stored_in,
    image_ref, diag_ref, gram_ref,
    tiles_ref, start_ref, previous_ref, stored_ref, load_sem,
    gathered, terms, pushed_in, own_out, own_in, half_in,
    corr_snd, corr_rcv, corr_full, raw_snd, raw_rcv, raw_full,
    image_half, image_other, gram_rcv,
    x_send, x_recv, p_send, p_recv, pair_send, pair_recv,
    cs_send, cs_recv, cg_send, cg_recv, rs_send, rs_recv, rg_send, rg_recv, g_send, g_recv,
):
    R, C, S = dims
    n = R * C * S
    r, c, s = lax.axis_index("rows"), lax.axis_index("cols"), lax.axis_index("sub")
    me = (r * C + c) * S + s
    block, rows = start_ref.shape
    half = rows // 2
    count = tiles_ref.shape[0]
    mine_k = stored_ref.shape[0]
    total_rows = rows * R * C
    inv_n = 1.0 / total_rows

    def dev(p):
        return {"rows": p // (C * S), "cols": (p // S) % C, "sub": p % S}

    def remote(src, dst, send, recv, target):
        return pltpu.make_async_remote_copy(
            src_ref=src, dst_ref=dst, send_sem=send, recv_sem=recv,
            device_id=target, device_id_type=MESH,
        )

    partner = {"rows": r, "cols": c, "sub": 1 - s}
    barrier = pltpu.get_barrier_semaphore()

    def greet(i):
        pl.semaphore_signal(barrier, inc=1, device_id=dev(lax.rem(me + i, n)), device_id_type=MESH)

    loads = [
        pltpu.make_async_copy(src, dst, load_sem.at[i])
        for i, (src, dst) in enumerate((
            (start_in, start_ref), (tiles_in, tiles_ref), (stored_in, stored_ref), (previous_in, previous_ref),
        ))
    ]
    for load in loads:
        load.start()
    loop(1, n, greet)

    for load in loads:
        load.wait()
    xt = start_ref[...]
    pt = previous_ref[...]
    xb = xt.astype(jnp.bfloat16)
    gathered[r] = xb
    first = s == 0

    def pick(v):
        return jnp.where(first, v[:, :half], v[:, half:])

    def pick_other(v):
        return jnp.where(first, v[:, half:], v[:, :half])

    pushed = [mm(xb, tiles_ref[k], NN) for k in range(count)]
    bands = [index_ref[k, 1] // C for k in range(count)]

    def term(band):
        total = jnp.where(bands[0] == band, pushed[0], 0.0)
        for k in range(1, count):
            total = total + jnp.where(bands[k] == band, pushed[k], 0.0)
        return total

    def fill(i):
        band = lax.rem(r + i, R)
        value = term(band).astype(jnp.bfloat16)
        terms[i, 0] = value[:, :half]
        terms[i, 1] = value[:, half:]

    loop(1, R, fill)
    pl.semaphore_wait(barrier, n - 1)

    def x_copy(i):
        return remote(gathered.at[r], gathered.at[r], x_send.at[i], x_recv.at[r],
                      {"rows": lax.rem(r + i, R), "cols": c, "sub": s})

    def p_copy(i, j):
        return remote(terms.at[i, j], pushed_in.at[r, s], p_send.at[i, j], p_recv.at[r, s],
                      {"rows": lax.rem(r + i, R), "cols": c, "sub": j})

    far = pl.ds(pl.multiple_of((1 - s) * half, LANES), half)
    pair0 = remote(stored_ref.at[:, :, far], half_in, pair_send.at[0], pair_recv.at[0], partner)
    pair0.start()
    loop(1, R, lambda i: x_copy(i).start())

    def push(i):
        p_copy(i, 0).start()
        p_copy(i, 1).start()

    loop(1, R, push)

    own_half = pick(stored_ref[...].reshape(mine_k * block, rows))
    x_half = pick(xt)
    p_half = pick(pt)
    x_split = split(x_half)
    row_id = lax.broadcasted_iota(jnp.int32, (block, block), 0)
    col_id = lax.broadcasted_iota(jnp.int32, (block, block), 1)
    upper = jnp.where(col_id >= row_id, coupling_ref[...], 0.0)
    base = pick(onsite_ref[...]) * x_half - dot3(split(upper), split(p_half), NN)

    def exchange(nch, snd, rcv, full, ssend, srecv, gsend, grecv):
        slots = (nch + n - 1) // n

        def scatter():
            for t in range(slots):
                if (t + 1) * n <= nch:
                    rcv[t, me] = snd[t * n + me]

                    def send(i):
                        p = lax.rem(me + i, n)
                        remote(snd.at[t * n + p], rcv.at[t, me], ssend.at[t * n + p],
                               srecv.at[t, me], dev(p)).start()

                    loop(1, n, send)
                else:
                    for ch in range(t * n, nch):
                        p = ch - t * n

                        @pl.when(me == p)
                        def _():
                            rcv[t, p] = snd[ch]

                        @pl.when(me != p)
                        def _():
                            remote(snd.at[ch], rcv.at[t, me], ssend.at[ch],
                                   srecv.at[t, me], dev(p)).start()

        def owned(t):
            return nch - t * n if (t + 1) * n > nch else n

        def gather_copy(t, i):
            p = lax.rem(me + i, n)
            return remote(full.at[t * n + me], full.at[t * n + me], gsend.at[t, i],
                          grecv.at[t * n + me], dev(p))

        def reduce_and_gather():
            for t in range(slots):
                def run():
                    def wait(i):
                        p = lax.rem(me + n - i, n)
                        remote(snd.at[0], rcv.at[t, p], ssend.at[0], srecv.at[t, p], dev(p)).wait_recv()

                    loop(1, n, wait)
                    full[t * n + me] = jnp.sum(rcv[t].astype(jnp.float32), axis=0)
                    loop(1, n, lambda i: gather_copy(t, i).start())

                if owned(t) == n:
                    run()
                else:
                    pl.when(me < owned(t))(run)

        def finish():
            for t in range(slots):
                if owned(t) == n:
                    def wait(i):
                        p = lax.rem(me + n - i, n)
                        remote(full.at[t * n + p], full.at[t * n + p], gsend.at[t, 0],
                               grecv.at[t * n + p], dev(p)).wait_recv()

                    loop(1, n, wait)
                else:
                    for p in range(owned(t)):
                        @pl.when(me != p)
                        def _():
                            remote(full.at[t * n + p], full.at[t * n + p], gsend.at[t, 0],
                                   grecv.at[t * n + p], dev(p)).wait_recv()

        def drain():
            for t in range(slots):
                if owned(t) == n:
                    def wait(i):
                        p = lax.rem(me + i, n)
                        remote(snd.at[t * n + p], rcv.at[t, me], ssend.at[t * n + p],
                               srecv.at[t, me], dev(p)).wait_send()
                        gather_copy(t, i).wait_send()

                    loop(1, n, wait)
                else:
                    for p in range(owned(t)):
                        @pl.when(me != p)
                        def _():
                            remote(snd.at[t * n + p], rcv.at[t, me], ssend.at[t * n + p],
                                   srecv.at[t, me], dev(p)).wait_send()

                    @pl.when(me < owned(t))
                    def _():
                        loop(1, n, lambda i: gather_copy(t, i).wait_send())

        return scatter, reduce_and_gather, finish, drain

    per = block // CH
    corr_n = corr_snd.shape[0]
    raw_n = raw_snd.shape[0]
    wide = corr_n // per
    pack = (raw_n - corr_n) // 2

    def put(snd, value):
        for kt in range(wide):
            for q in range(per):
                snd[kt * per + q] = value[q * CH:(q + 1) * CH, kt * LANES:(kt + 1) * LANES].astype(snd.dtype)

    def take(full):
        parts = [jnp.concatenate([full[kt * per + q] for q in range(per)], axis=0) for kt in range(wide)]
        return jnp.concatenate(parts, axis=1)

    corr = exchange(corr_n, corr_snd, corr_rcv, corr_full, cs_send, cs_recv, cg_send, cg_recv)
    raw = exchange(raw_n, raw_snd, raw_rcv, raw_full, rs_send, rs_recv, rg_send, rg_recv)

    pair0.wait_recv()
    other_half = half_in[...].reshape(mine_k * block, half)
    both = jnp.concatenate([jnp.where(first, own_half, other_half), jnp.where(first, other_half, own_half)], axis=0)
    basis = split(both)
    put(corr_snd, dot3(x_split, basis, NT))
    corr[0]()

    def x_wait(i):
        p = lax.rem(r + R - i, R)
        remote(gathered.at[p], gathered.at[p], x_send.at[i], x_recv.at[p], partner).wait_recv()

    loop(1, R, x_wait)
    own = term(r)
    for k in range(count):
        own = own + mm(gathered[bands[k]], tiles_ref[k], NT)
    own_out[...] = pick_other(own)
    pair1 = remote(own_out, own_in, pair_send.at[1], pair_recv.at[1], partner)
    pair1.start()
    w = base + pick(own)

    def p_wait(i):
        p = lax.rem(r + R - i, R)
        for j in range(S):
            remote(terms.at[1, j], pushed_in.at[p, j], p_send.at[1, j], p_recv.at[p, j], partner).wait_recv()

    loop(1, R, p_wait)
    pushed_in[r] = jnp.zeros((S, block, half), jnp.bfloat16)
    received = jnp.sum(pushed_in[...].astype(jnp.float32), axis=(0, 1))
    pair1.wait_recv()
    w = w + (received + own_in[...])
    w_split = split(w)
    put(raw_snd, dot3(w_split, basis, NT))
    diag_part = dot3(w_split, x_split, NT)
    packed = jnp.concatenate([diag_part[:block // 2], diag_part[block // 2:]], axis=1)
    for h, part in enumerate(split(packed)):
        for q in range(pack):
            raw_snd[corr_n + h * pack + q] = part[q * CH:(q + 1) * CH]
    raw[0]()
    corr[1]()
    raw[1]()
    corr[2]()
    x_clean = x_half - dot3(split(take(corr_full) * inv_n), basis, NN)
    x_clean = split(x_clean)
    raw[2]()
    packed = jnp.concatenate([raw_full[corr_n + q] + raw_full[corr_n + pack + q] for q in range(pack)], axis=0) * inv_n
    diag_t = jnp.concatenate([packed[:, :block], packed[:, block:]], axis=0)
    w = w - (dot3(split(take(raw_full) * inv_n), basis, NN) + dot3(split(diag_t), x_clean, NN))
    image_half[...] = w
    pair2 = remote(image_half, image_other, pair_send.at[2], pair_recv.at[2], partner)
    pair2.start()
    zero = jnp.zeros((block, block), jnp.float32)
    square = jnp.concatenate([diag_t, zero], axis=1)
    square = jnp.concatenate([square, jnp.zeros_like(square)], axis=0).T
    diag_ref[...] = square[:block, :block]
    pair2.wait_recv()
    other = image_other[...]
    images = jnp.concatenate([jnp.where(first, w, other), jnp.where(first, other, w)], axis=1)
    image_ref[...] = images
    images = split(images)
    gram = dot3(images, images, NT)
    spot = r * C + c
    peers = R * C
    packed = jnp.concatenate([gram[:block // 2], gram[block // 2:]], axis=1)
    gram_rcv[spot] = packed

    def g_copy(i):
        p = lax.rem(spot + i, peers)
        return remote(gram_rcv.at[spot], gram_rcv.at[spot], g_send.at[i], g_recv.at[spot],
                      {"rows": p // C, "cols": p % C, "sub": s})

    loop(1, peers, lambda i: g_copy(i).start())

    def g_wait(i):
        p = lax.rem(spot + peers - i, peers)
        remote(gram_rcv.at[p], gram_rcv.at[p], g_send.at[i], g_recv.at[p], partner).wait_recv()

    loop(1, peers, g_wait)
    packed = jnp.sum(gram_rcv[...], axis=0) * inv_n
    gram = jnp.concatenate([packed[:, :block], packed[:, block:]], axis=0)

    gram_ref[...] = gram
    pair0.wait_send()
    pair1.wait_send()
    pair2.wait_send()

    def sent(i):
        x_copy(i).wait_send()
        p_copy(i, 0).wait_send()
        p_copy(i, 1).wait_send()

    loop(1, R, sent)
    corr[3]()
    raw[3]()
    loop(1, peers, lambda i: g_copy(i).wait_send())


def finish_kernel(image_ref, diag_in, gram_ref, new_ref, diag_ref, coup_ref):
    block = gram_ref.shape[0]
    row_id = lax.broadcasted_iota(jnp.int32, (block, block), 0)
    col_id = lax.broadcasted_iota(jnp.int32, (block, block), 1)
    eye = jnp.where(row_id == col_id, 1.0, 0.0)
    full = eliminate(jnp.concatenate([gram_ref[...], eye], axis=1), block)
    coup_ref[0] = jnp.where(col_id >= row_id, full[:, :block], 0.0)
    diag_ref[0] = diag_in[...]
    inverse = split(jnp.where(col_id <= row_id, full[:, block:], 0.0))
    new_ref[0] = dot3(inverse, split(image_ref[...]), NN)


def solution(mesh):
    R, C, S = mesh.shape["rows"], mesh.shape["cols"], mesh.shape["sub"]
    n = R * C * S

    def local(index, tiles, onsite, start, previous, coupling, stored):
        rows, block = start.shape
        tile = tiles.shape[1]
        assert rows == tile and S == 2 and 2 * block == LANES
        half = rows // 2
        mine = stored.shape[0] * block
        corr_n = (S * mine // LANES) * (block // CH)
        raw_n = corr_n + 2 * block * block // (CH * LANES)
        f32, bf16 = jnp.float32, jnp.bfloat16
        dma = pltpu.SemaphoreType.DMA

        def ring(nch, kind):
            slots = -(-nch // n)
            return [
                pltpu.VMEM((nch, CH, LANES), kind),
                pltpu.VMEM((slots, n, CH, LANES), kind),
                pltpu.VMEM((nch, CH, LANES), f32),
            ]

        def ring_sems(nch):
            slots = -(-nch // n)
            return [dma((nch,)), dma((slots, n)), dma((slots, n)), dma((nch,))]

        vmem = pl.BlockSpec(memory_space=pltpu.VMEM)
        hbm = pl.BlockSpec(memory_space=pl.ANY)
        image, diagonal, gram = pl.pallas_call(
            functools.partial(kernel, (R, C, S)),
            out_shape=(
                jax.ShapeDtypeStruct((block, rows), f32),
                jax.ShapeDtypeStruct((block, block), f32),
                jax.ShapeDtypeStruct((block, block), f32),
            ),
            in_specs=[pl.BlockSpec(memory_space=pltpu.SMEM), hbm, vmem, hbm, hbm, vmem, hbm],
            out_specs=(vmem, vmem, vmem),
            scratch_shapes=[
                pltpu.VMEM(tiles.shape, tiles.dtype),
                pltpu.VMEM((block, rows), f32),
                pltpu.VMEM((block, rows), f32),
                pltpu.VMEM((mine // block, block, rows), f32),
                dma((4,)),
                pltpu.VMEM((R, block, rows), bf16),
                pltpu.VMEM((R, S, block, half), bf16),
                pltpu.VMEM((R, S, block, half), bf16),
                pltpu.VMEM((block, half), f32),
                pltpu.VMEM((block, half), f32),
                pltpu.VMEM((mine // block, block, half), f32),
                *ring(corr_n, f32),
                *ring(raw_n, bf16),
                pltpu.VMEM((block, half), f32),
                pltpu.VMEM((block, half), f32),
                pltpu.VMEM((R * C, block // 2, LANES), f32),
                dma((R,)), dma((R,)), dma((R, S)), dma((R, S)), dma((3,)), dma((3,)),
                *ring_sems(corr_n),
                *ring_sems(raw_n),
                dma((R * C,)), dma((R * C,)),
            ],
            compiler_params=pltpu.CompilerParams(collective_id=0, has_side_effects=True),
        )(index, tiles, onsite.reshape(1, rows), start.T, previous.T, coupling, stored.transpose(0, 2, 1))
        new, diagonal, upper = pl.pallas_call(
            finish_kernel,
            out_shape=(
                jax.ShapeDtypeStruct((1, block, rows), f32),
                jax.ShapeDtypeStruct((1, block, block), f32),
                jax.ShapeDtypeStruct((1, block, block), f32),
            ),
            in_specs=[vmem] * 3,
            out_specs=(vmem, vmem, vmem),
        )(image, diagonal, gram)
        return new.transpose(0, 2, 1), diagonal, upper

    return jax.shard_map(
        local,
        mesh=mesh,
        in_specs=(
            P(("groups", "rows", "cols", "sub"), None),
            P(("groups", "rows", "cols", "sub"), None, None),
            P(("groups", "rows", "cols")),
            P(("groups", "rows", "cols"), None),
            P(("groups", "rows", "cols"), None),
            P("groups", None),
            P("sub", ("groups", "rows", "cols"), None),
        ),
        out_specs=(
            P(None, ("groups", "rows", "cols"), None),
            P(None, "groups", None),
            P(None, "groups", None),
        ),
        check_vma=False,
    )
```

time: 218 us -> 40.8 us (0.19)
  blocking collectives: 90.4 us -> 0 us
  waiting for transfers between devices: 71.9 us -> 0 us
  Pallas kernels: 0 us -> 39.9 us
  matrix products: 17.8 us -> 0 us
  other arithmetic: 15.4 us -> 0 us
  between operations: 13.9 us -> 0.64 us
  local copies, waits for them, and re-layouts: 8.02 us -> 0 us
    psum x2 -> x0, blocking collectives: 74.8 us -> none  [the longest x1 37.4 us: local(): gram = lax.psum(gram_local, ('rows', 'cols')) / total_rows]
    psum x3 -> x0, waiting for transfers between devices: 71.9 us -> none  [the longest x1 36.2 us: local(): correlation = lax.psum(correlation_local, ('rows', 'cols')) / total_rows]
    pallas_call x0 -> x2, Pallas kernels: none -> 39.9 us  [the longest x1 36.2 us: local(): pl.pallas_call(functools.partial(kernel, (R, C, S)), out_shape=(jax.Shape...]
    dot_general x12 -> x0, matrix products: 16.9 us -> none  [the longest x1 8.95 us: apply_operator(): jnp.einsum('tk,kan->tan', row_onehot, pulled, precision=highest)]
    all_gather x1 -> x0, blocking collectives: 15.6 us -> none  [apply_operator(): gathered = lax.all_gather(own_tiles, 'rows', axis=0, tiled=True)]
    another operation x6 -> x0, other arithmetic: 12.1 us -> none  [the longest x3 6.52 us: local(): lower_factor = jnp.linalg.cholesky(gram)]
    dot_general x2 -> x0, local copies, waits for them, and re-layouts: 5.95 us -> none  [the longest x1 5.19 us: apply_operator(): jnp.einsum('tk,kan->tan', row_onehot, pulled, precision=highest)]
  transfers between devices with their start and end apart: 4 -> 0, of which waited for: 3 -> 0; matrix products, arithmetic and copies ran while one was open for 8% -> 0% of each run, Pallas kernels for 0% -> 0%
where the time goes in v1:
time: 40.8 us; the launch traced here: 40.6 us
  Pallas kernels  39.9 us (98%)
  between operations  0.64 us (2%)
    pallas_call x1, Pallas kernels, local(): pl.pallas_call(functools.partial(kernel, (R, C, S)), out_shape=(jax.Shape...  36.2 us
    pallas_call x1, Pallas kernels, local(): pl.pallas_call(finish_kernel, out_shape=(jax.ShapeDtypeStruct((1, block,...  3.7 us

profile of v1, /device:TPU:0, one launch (start us, length us, event | category | flops | bytes accessed | tf_op | source)
XLA Modules:
  0.0 40.6 jit_solution(6720905037633926139)
XLA Ops:
  0.6 36.2 %shard_map.94 = (f32[64,256]{1,0:T(8,128)}, f32[64,64]{1,0:T(8,128)}, f32[64,64]{1,0:T(8,128)}) custom-call(s32[2,2]{1,0:T(2,128)} %index_ref.1, bf16[2,256,256]{2,1,0:T(8,128)(2,1)} %tiles_in.1, f32[1,256]{1,0:T(1,128)} %bitcast.8, f32[64,256]{1,0:T(8,128)} %bitcast.6, f32[64,256]{1,0:T(8,128)} %bitcast.7, f32[64,64]{1,0:T(8,128)} %coupling_ref.1, ...), custom_call_target="tpu_custom_call" | custom-call | tf_op jit(solution)/shard_map/pallas_call | solution.py:422
  36.9 3.7 %shard_map.95 = (f32[1,64,256]{2,1,0:T(8,128)}, f32[1,64,64]{2,1,0:T(8,128)}, f32[1,64,64]{2,1,0:T(8,128)}) custom-call(f32[64,256]{1,0:T(8,128)} %get-tuple-element.9.image_ref, f32[64,64]{1,0:T(8,128)} %get-tuple-element.10.diag_in, f32[64,64]{1,0:T(8,128)} %get-tuple-element.11.gram_ref), custom_call_target="tpu_custom_call" | custom-call | tf_op jit(solution)/shard_map/pallas_call | solution.py:455
